TPU v7x, 8 devices: a whole 2x2x1 slice. The times are simulated.
8 devices in a mesh: dp: 2 (over z, y), tp: 4 (over x, core).
Axes of the slice: x: 2, y: 2, z: 1, core: 2. Of those that a mesh axis runs over, the one named last changes fastest.
Arguments:
- x: bfloat16 [640, 3072], P('dp'), parts along dimension 0
- lengths: int32 [130], P('dp'), parts along dimension 0
- attn_gain: bfloat16 [2, 3072], replicated
- w_q: bfloat16 [2, 3072, 3072], P(None, None, 'tp')
- w_k: bfloat16 [2, 3072, 1024], P(None, None, 'tp')
- w_v: bfloat16 [2, 3072, 1024], P(None, None, 'tp')
- w_o: bfloat16 [2, 3072, 3072], P(None, 'tp')
- mlp_gain: bfloat16 [2, 3072], replicated
- w_gate: bfloat16 [2, 3072, 8192], P(None, None, 'tp')
- w_up: bfloat16 [2, 3072, 8192], P(None, None, 'tp')
- w_down: bfloat16 [2, 8192, 3072], P(None, 'tp')
- k_cache: bfloat16 [2, 130, 8, 1024, 128], P(None, 'dp', 'tp'), parts along dimension 1
- v_cache: bfloat16 [2, 130, 8, 1024, 128], P(None, 'dp', 'tp'), parts along dimension 1
Outputs:
- output: bfloat16 [640, 3072], P('dp'), parts along dimension 0
There are 2 independent parts. A program takes and returns all parts, laid end to end along the dimension named above; an argument that names none is the same for every part.
All inputs are finite; a program needn't handle non-finite values.
Results may differ from a plain program's by a relative error of at most 0.0197503.
Values are sent between devices in bfloat16 or wider.
A program may use at most 1 GiB of HBM per device.

v0:
```python
import functools
import math

import jax
import jax.numpy as jnp
from jax import lax
from jax.experimental import pallas as pl
from jax.experimental.pallas import tpu as pltpu
from jax.sharding import PartitionSpec as P

ROPE_BASE = 500000.0
EPSILON = 1e-5
MESH = pl.DeviceIdType.MESH
F32 = jnp.float32
BF16 = jnp.bfloat16
VMEM_LIMIT = 64_600_000
TILE = 256
DOWN_TILE = 512
SLOTS = 3
GROUPS = ((0, 112), (112, 112), (224, 96))


def rope_tables(len_ref, cos_ref, sin_ref):
    rows, head = cos_ref.shape
    dec_rows = len_ref.shape[0] - 1
    block = 8
    lane = lax.broadcasted_iota(jnp.int32, (block, head), 1)
    sub = lax.broadcasted_iota(jnp.int32, (block, head), 0)
    freq = jnp.exp(lax.rem(lane, head // 2).astype(F32) * (-2.0 / head * math.log(ROPE_BASE)))
    sign = jnp.where(lane < head // 2, -1.0, 1.0)

    def put(i, position):
        at = pl.ds(pl.multiple_of(i * block, block), block)
        angle = position.astype(F32) * freq
        cos_ref[at, :] = jnp.cos(angle)
        sin_ref[at, :] = jnp.sin(angle) * sign

    def decode(i, _):
        position = jnp.zeros((block, head), jnp.int32)
        for r in range(block):
            position = jnp.where(sub == r, len_ref[i * block + r], position)
        put(i, position)
        return 0

    def prefill(i, _):
        put(i, sub + (i * block - dec_rows + len_ref[dec_rows]))
        return 0

    lax.fori_loop(0, dec_rows // block, decode, 0)
    lax.fori_loop(dec_rows // block, rows // block, prefill, 0)


def norm_rows(h_ref, gain, b_ref, row0, rows, block=16):
    half = h_ref.shape[2]
    gain_lo, gain_hi = gain[:, :half], gain[:, half:]

    def step(i, _):
        src = pl.ds(pl.multiple_of(row0 + i * block, block), block)
        dst = pl.ds(pl.multiple_of(i * block, block), block)
        lo, hi = h_ref[0, src, :].astype(F32), h_ref[1, src, :].astype(F32)
        total = jnp.sum(lo * lo, axis=-1, keepdims=True) + jnp.sum(hi * hi, axis=-1, keepdims=True)
        inv = lax.rsqrt(total / (2 * half) + EPSILON)
        b_ref[dst, :half] = (lo * inv * gain_lo).astype(BF16)
        b_ref[dst, half:] = (hi * inv * gain_hi).astype(BF16)
        return 0

    lax.fori_loop(0, rows // block, step, 0)


def rope_store(prod, cos, sin, out_ref, rows, col):
    head = cos.shape[1]
    for k in range(prod.shape[1] // head):
        vec = prod[:, k * head:(k + 1) * head].astype(BF16).astype(F32)
        rot = vec * cos + pltpu.roll(vec, head // 2, 1) * sin
        out_ref[rows, pl.ds(col + k * head, head)] = rot.astype(BF16)


def qkv_rows(b_ref, wq_ref, wk_ref, wv_ref, cos_ref, sin_ref, q_ref, k_ref, v_ref, row0, rows):
    rows_at = pl.ds(row0, rows)
    lhs = b_ref[0:rows, :]
    cos, sin = cos_ref[rows_at, :], sin_ref[rows_at, :]

    def q_tile(j, _):
        col = pl.multiple_of(j * TILE, TILE)
        prod = jnp.dot(b_ref[0:rows, :], wq_ref[:, pl.ds(col, TILE)], preferred_element_type=F32)
        rope_store(prod, cos_ref[rows_at, :], sin_ref[rows_at, :], q_ref, rows_at, col)
        return 0

    lax.fori_loop(0, wq_ref.shape[1] // TILE, q_tile, 0)
    rope_store(jnp.dot(lhs, wk_ref[...], preferred_element_type=F32), cos, sin, k_ref, rows_at, 0)
    v_ref[rows_at, :] = jnp.dot(lhs, wv_ref[...], preferred_element_type=F32).astype(BF16)


def qkv_kernel(len_ref, x_hbm, gain_ref, wq_hbm, wk_hbm, wv_hbm, q_ref, k_ref, v_ref, cos_ref, sin_ref, h, b, wq, wk, wv, sems):
    half = h.shape[2]
    copies = [pltpu.make_async_copy(x_hbm.at[:, pl.ds(s * half, half)], h.at[s], sems.at[s]) for s in range(2)]
    copies += [pltpu.make_async_copy(src.at[0], dst, sems.at[2 + n]) for n, (src, dst) in enumerate(((wq_hbm, wq), (wk_hbm, wk), (wv_hbm, wv)))]
    for copy in copies:
        copy.start()
    rope_tables(len_ref, cos_ref, sin_ref)
    copies[0].wait()
    copies[1].wait()
    rows = h.shape[1]
    norm_rows(h, gain_ref[...].astype(F32)[0:1, :], b, 0, rows)
    for copy in copies[2:]:
        copy.wait()
    qkv_rows(b, wq, wk, wv, cos_ref, sin_ref, q_ref, k_ref, v_ref, 0, rows)


def qkv_call(lengths, x, gain, w_q, w_k, w_v, head):
    rows, width = x.shape
    vmem = pl.BlockSpec(memory_space=pltpu.VMEM)
    hbm = pl.BlockSpec(memory_space=pl.ANY)
    return pl.pallas_call(
        qkv_kernel,
        name='qkv_first',
        out_shape=[jax.ShapeDtypeStruct((rows, w.shape[2]), BF16) for w in (w_q, w_k, w_v)] + [jax.ShapeDtypeStruct((rows, head), F32)] * 2,
        in_specs=[pl.BlockSpec(memory_space=pltpu.SMEM), hbm, vmem, hbm, hbm, hbm],
        out_specs=[vmem] * 5,
        scratch_shapes=[
            pltpu.VMEM((2, rows, width // 2), BF16),
            pltpu.VMEM((rows, width), BF16),
            pltpu.VMEM(w_q.shape[1:], BF16),
            pltpu.VMEM(w_k.shape[1:], BF16),
            pltpu.VMEM(w_v.shape[1:], BF16),
            pltpu.SemaphoreType.DMA((5,)),
        ],
        compiler_params=pltpu.CompilerParams(vmem_limit_bytes=61 * 2**20),
    )(lengths, x, gain, w_q, w_k, w_v)


BATCH = 8
SPAN = 256


def length_order(lengths):
    ids = jnp.arange(lengths.shape[0], dtype=jnp.int32)
    lengths = jnp.where(ids == lengths.shape[0] - 1, 0, lengths)
    mine, other = lengths[:, None], lengths[None, :]
    ahead = (other > mine) | ((other == mine) & (ids[None, :] < ids[:, None]))
    rank = jnp.sum(ahead.astype(jnp.int32), axis=1)
    return jnp.sum(jnp.where(rank[None, :] == ids[:, None], ids[None, :], 0), axis=1)


def attention_kernel(layer, len_ref, order_ref, q_hbm, k_hbm, v_hbm, kc_hbm, vc_hbm, o_ref, q_ref, k_ref, v_ref, kbuf, vbuf, qs, kf, vf, sc, od, kp, vp, sems, psems):
    rows = kc_hbm.shape[1] - 1
    seq, head = kc_hbm.shape[3], kc_hbm.shape[4]
    heads = q_ref.shape[1] // head
    kv = kc_hbm.shape[2]
    rep = heads // kv
    scale = head ** -0.5
    steps = rows // BATCH
    spans = seq // SPAN
    nt = (((1,), (1,)), ((), ()))

    def step_spans(step):
        return len_ref[order_ref[step * BATCH]] // SPAN + 1

    def copies(step, slot, n, act):
        at = pl.ds(0, n * SPAN)
        for i in range(BATCH):
            row = order_ref[step * BATCH + i]
            for m, (src, dst) in enumerate(((kc_hbm, kbuf), (vc_hbm, vbuf))):
                copy = pltpu.make_async_copy(src.at[layer, row, :, at, :], dst.at[slot, i, :, at, :], sems.at[slot, i, m])
                if act == 'start':
                    copy.start()
                else:
                    copy.wait()

    def fetch(step, slot):
        for n in range(1, spans + 1):
            @pl.when(step_spans(step) == n)
            def _(n=n):
                copies(step, slot, n, 'start')

    fresh = [pltpu.make_async_copy(src, dst, psems.at[2 + n]) for n, (src, dst) in enumerate(((q_hbm, q_ref), (k_hbm, k_ref), (v_hbm, v_ref)))]
    for copy in fresh:
        copy.start()
    prefill = [pltpu.make_async_copy(src.at[layer, rows], dst, psems.at[n]) for n, (src, dst) in enumerate(((kc_hbm, kp), (vc_hbm, vp)))]
    for copy in prefill:
        copy.start()
    for step in range(SLOTS - 1):
        fetch(step, step)

    qs[...] = jnp.zeros_like(qs)
    for copy in fresh:
        copy.wait()
    for h in range(heads):
        qs[h // rep, pl.ds(h, rows, stride=8), :] = q_ref[0:rows, h * head:(h + 1) * head].astype(F32)
    kf[...] = k_ref[0:rows, :].astype(F32)
    vf[...] = v_ref[0:rows, :].astype(F32)

    for copy in prefill:
        copy.wait()
    limit = len_ref[rows]

    def prefill_head(h, _, keys):
        g = h // rep
        q = q_ref[rows:, pl.ds(pl.multiple_of(h * head, head), head)]
        kn = k_ref[rows:, pl.ds(pl.multiple_of(g * head, head), head)]
        vn = v_ref[rows:, pl.ds(pl.multiple_of(g * head, head), head)]
        s_old = lax.dot_general(q, kp[g, 0:keys, :], nt, preferred_element_type=F32) * scale
        s_new = lax.dot_general(q, kn, nt, preferred_element_type=F32) * scale
        s_old = jnp.where(lax.broadcasted_iota(jnp.int32, s_old.shape, 1) < limit, s_old, -jnp.inf)
        causal = lax.broadcasted_iota(jnp.int32, s_new.shape, 1) <= lax.broadcasted_iota(jnp.int32, s_new.shape, 0)
        s_new = jnp.where(causal, s_new, -jnp.inf)
        top = jnp.maximum(jnp.max(s_old, axis=-1, keepdims=True), jnp.max(s_new, axis=-1, keepdims=True))
        e_old, e_new = jnp.exp(s_old - top), jnp.exp(s_new - top)
        inv = 1.0 / (jnp.sum(e_old, axis=-1, keepdims=True) + jnp.sum(e_new, axis=-1, keepdims=True))
        out = jnp.dot((e_old * inv).astype(BF16), vp[g, 0:keys, :], preferred_element_type=F32)
        out += jnp.dot((e_new * inv).astype(BF16), vn, preferred_element_type=F32)
        o_ref[rows:, pl.ds(pl.multiple_of(h * head, head), head)] = out.astype(BF16)
        return 0

    for n in range(1, spans + 1):
        @pl.when((limit + SPAN - 1) // SPAN == n)
        def _(n=n):
            lax.fori_loop(0, heads, functools.partial(prefill_head, keys=n * SPAN), 0)

    def attend(step, slot, n):
        keys = n * SPAN
        copies(step, slot, n, 'wait')
        for i in range(BATCH):
            row = order_ref[step * BATCH + i]
            length = len_ref[row]
            base = pl.multiple_of((length // 16) * 16, 16)
            hit = lax.broadcasted_iota(jnp.int32, (16, head), 0) == length - base
            near = pl.ds(pl.multiple_of((row // 8) * 8, 8), 8)
            pick = lax.broadcasted_iota(jnp.int32, (8, head), 0) == lax.rem(row, 8)
            for buf, new in ((kbuf, kf), (vbuf, vf)):
                for g in range(kv):
                    old = buf[slot, i, g, pl.ds(base, 16), :].astype(F32)
                    mine = jnp.sum(jnp.where(pick, new[near, g * head:(g + 1) * head], 0.0), axis=0, keepdims=True)
                    buf[slot, i, g, pl.ds(base, 16), :] = jnp.where(hit, mine, old).astype(BF16)
        for i in range(BATCH):
            row = order_ref[step * BATCH + i]
            at = pl.ds(pl.multiple_of(row * 8, 8), 8)
            q = jnp.concatenate([qs[g, at, :] for g in range(kv)], axis=-1).astype(BF16)
            key = jnp.concatenate([kbuf[slot, i, g, 0:keys, :] for g in range(kv)], axis=-1)
            s = lax.dot_general(q, key, nt, preferred_element_type=F32) * scale
            s = jnp.where(lax.broadcasted_iota(jnp.int32, s.shape, 1) <= len_ref[row], s, -jnp.inf)
            sc[i * 8:(i + 1) * 8, 0:keys] = s
        for i in range(BATCH):
            s = sc[i * 8:(i + 1) * 8, 0:keys]
            e = jnp.exp(s - jnp.max(s, axis=-1, keepdims=True))
            p = (e * (1.0 / jnp.sum(e, axis=-1, keepdims=True))).astype(BF16)
            value = jnp.concatenate([vbuf[slot, i, g, 0:keys, :] for g in range(kv)], axis=-1)
            o = jnp.dot(p, value, preferred_element_type=F32)
            own = lax.broadcasted_iota(jnp.int32, (8, head), 0) // rep
            pick = o[:, 0:head]
            for g in range(1, kv):
                pick = jnp.where(own == g, o[:, g * head:(g + 1) * head], pick)
            row = order_ref[step * BATCH + i]
            od[pl.ds(pl.multiple_of(row * 8, 8), 8), :] = pick

    def decode_step(step, _):
        slot = lax.rem(step, SLOTS)

        @pl.when(step + SLOTS - 1 < steps)
        def _():
            fetch(step + SLOTS - 1, lax.rem(step + SLOTS - 1, SLOTS))

        for n in range(1, spans + 1):
            @pl.when(step_spans(step) == n)
            def _(n=n):
                attend(step, slot, n)
        return 0

    lax.fori_loop(0, steps, decode_step, 0)
    for h in range(heads):
        o_ref[0:rows, h * head:(h + 1) * head] = od[pl.ds(h, rows, stride=8), :].astype(BF16)


def attention_call(layer, lengths, order, q, k, v, k_cache, v_cache):
    rows = k_cache.shape[1] - 1
    kv, seq, head = k_cache.shape[2:]
    vmem = pl.BlockSpec(memory_space=pltpu.VMEM)
    hbm = pl.BlockSpec(memory_space=pl.ANY)
    return pl.pallas_call(
        functools.partial(attention_kernel, layer),
        name=f'attention_{layer}',
        out_shape=jax.ShapeDtypeStruct(q.shape, BF16),
        in_specs=[pl.BlockSpec(memory_space=pltpu.SMEM)] * 2 + [hbm] * 5,
        out_specs=vmem,
        scratch_shapes=[
            pltpu.VMEM(q.shape, BF16),
            pltpu.VMEM(k.shape, BF16),
            pltpu.VMEM(v.shape, BF16),
            pltpu.VMEM((SLOTS, BATCH, kv, seq, head), BF16),
            pltpu.VMEM((SLOTS, BATCH, kv, seq, head), BF16),
            pltpu.VMEM((kv, rows * 8, head), F32),
            pltpu.VMEM((rows, kv * head), F32),
            pltpu.VMEM((rows, kv * head), F32),
            pltpu.VMEM((BATCH * 8, seq), F32),
            pltpu.VMEM((rows * 8, head), F32),
            pltpu.VMEM((kv, seq, head), BF16),
            pltpu.VMEM((kv, seq, head), BF16),
            pltpu.SemaphoreType.DMA((SLOTS, BATCH, 2)),
            pltpu.SemaphoreType.DMA((5,)),
        ],
        compiler_params=pltpu.CompilerParams(vmem_limit_bytes=60 * 2**20),
    )(lengths, order, q, k, v, k_cache, v_cache)


def block_kernel(layer, last, groups, *refs):
    if last:
        (x_hbm, att_hbm, gain_ref, wo_hbm, wg_hbm, wu_hbm, wd_hbm, out_ref,
         xh, att, h, part, got, send, cross, b, act, wo, wg, wu, wd, lsem, osem, msem, csem, fsem) = refs
    else:
        (x_hbm, att_hbm, gain_ref, wo_hbm, wg_hbm, wu_hbm, wd_hbm, next_gain_ref, cos_hbm, sin_hbm, wq_hbm, wk_hbm, wv_hbm, out_ref, q_hbm, k_hbm, v_hbm,
         xh, att, h, part, got, send, cross, b, act, wo, wg, wu, wd, wq, wk, wv, cos_ref, sin_ref, q_ref, k_ref, v_ref, lsem, osem, msem, csem, fsem) = refs
    tp = lax.axis_index('tp')
    core = lax.rem(tp, 2)
    mate = tp + 1 - 2 * core
    peer = lax.rem(tp + 2, 4)
    half = h.shape[2]
    own_cols = pl.ds(pl.multiple_of(core * half, half), half)

    loads = [(x_hbm.at[:, own_cols], xh), (att_hbm, att), (wo_hbm.at[layer], wo), (wg_hbm.at[layer], wg), (wu_hbm.at[layer], wu), (wd_hbm.at[layer], wd)]
    if not last:
        loads += [(wq_hbm.at[layer + 1], wq), (wk_hbm.at[layer + 1], wk), (wv_hbm.at[layer + 1], wv), (cos_hbm, cos_ref), (sin_hbm, sin_ref)]
    loads = [pltpu.make_async_copy(src, dst, lsem.at[n]) for n, (src, dst) in enumerate(loads)]
    order = [1, 2, 0] + list(range(3, len(loads)))
    for n in order:
        loads[n].start()

    barrier = pltpu.get_barrier_semaphore()
    for other in (mate, peer):
        pl.semaphore_signal(barrier, inc=1, device_id={'tp': other}, device_id_type=MESH)
    pl.semaphore_wait(barrier, 2)

    def remote(src, dst, sem, idx, device):
        return pltpu.make_async_remote_copy(src_ref=src, dst_ref=dst, send_sem=sem.at[0, idx[0], idx[1]], recv_sem=sem.at[1, idx[0], idx[1]], device_id={'tp': device}, device_id_type=MESH)

    def to_mate(phase, g):
        at = pl.ds(*groups[g])
        return remote(part.at[1 - core, at], got.at[at], msem, (phase, g), mate)

    def to_peer(phase, g):
        at = pl.ds(*groups[g])
        return remote(send.at[at], cross.at[phase, at], csem, (phase, g), peer)

    def final(phase, g):
        at = pl.ds(*groups[g])
        return remote(h.at[core, at], h.at[core, at], fsem, (phase, g), mate)

    def project(lhs_ref, lhs_at, w_ref, g):
        row0, rows = groups[g]
        per_half = half // DOWN_TILE

        def tile(j, _):
            col = pl.multiple_of(j * DOWN_TILE, DOWN_TILE)
            prod = jnp.dot(lhs_ref[lhs_at, :], w_ref[:, pl.ds(col, DOWN_TILE)], preferred_element_type=F32)
            side = j // per_half
            part[side, pl.ds(row0, rows), pl.ds(pl.multiple_of((j - side * per_half) * DOWN_TILE, DOWN_TILE), DOWN_TILE)] = prod.astype(BF16)
            return 0

        lax.fori_loop(0, 2 * per_half, tile, 0, unroll=2)

    def chip_sum(g):
        row0, rows = groups[g]

        def step(i, _):
            at = pl.ds(pl.multiple_of(row0 + i * 16, 16), 16)
            send[at, :] = (part[core, at, :].astype(F32) + got[at, :].astype(F32)).astype(BF16)
            return 0

        lax.fori_loop(0, rows // 16, step, 0)

    def add_sum(phase, g):
        row0, rows = groups[g]

        def step(i, _):
            at = pl.ds(pl.multiple_of(row0 + i * 16, 16), 16)
            base = xh[at, :] if phase == 0 else h[core, at, :]
            total = send[at, :].astype(F32) + cross[phase, at, :].astype(F32)
            h[core, at, :] = (base.astype(F32) + total).astype(BF16)
            return 0

        lax.fori_loop(0, rows // 16, step, 0)

    count = len(groups)

    def arrive(phase, g):
        to_peer(phase, g).wait()
        add_sum(phase, g)
        final(phase, g).start()

    def leave(phase, g):
        to_mate(phase, g).wait()
        chip_sum(g)
        to_peer(phase, g).start()

    loads[1].wait()
    loads[2].wait()
    for g in range(count):
        project(att, pl.ds(*groups[g]), wo, g)
        to_mate(0, g).start()
        if g > 0:
            leave(0, g - 1)
    leave(0, count - 1)
    loads[0].wait()
    mlp_gain = gain_ref[...].astype(F32)[layer:layer + 1, :]
    arrive(0, 0)
    for g in range(count):
        row0, rows = groups[g]
        final(0, g).wait()
        norm_rows(h, mlp_gain, b, row0, rows)
        if g == 0:
            loads[3].wait()
            loads[4].wait()

        def up_tile(j, _, rows=rows):
            cols = pl.ds(pl.multiple_of(j * TILE, TILE), TILE)
            gate = jnp.dot(b[0:rows, :], wg[:, cols], preferred_element_type=F32)
            up = jnp.dot(b[0:rows, :], wu[:, cols], preferred_element_type=F32)
            act[0:rows, cols] = (gate * (1.0 / (1.0 + jnp.exp(-gate))) * up).astype(BF16)
            return 0

        lax.fori_loop(0, wg.shape[1] // TILE, up_tile, 0, unroll=2)
        if g == 0:
            loads[5].wait()
        project(act, pl.ds(0, rows), wd, g)
        to_mate(1, g).start()
        if g + 1 < count:
            arrive(0, g + 1)
        leave(1, g)
    if not last:
        next_gain = next_gain_ref[...].astype(F32)[layer + 1:layer + 2, :]
        for n in range(6, len(loads)):
            loads[n].wait()
    outs = []
    for g in range(len(groups)):
        row0, rows = groups[g]
        arrive(1, g)
        final(1, g).wait()
        at = pl.ds(row0, rows)
        moves = [(h.at[s, at], out_ref.at[at, pl.ds(s * half, half)]) for s in range(2)]
        if not last:
            norm_rows(h, next_gain, b, row0, rows)
            qkv_rows(b, wq, wk, wv, cos_ref, sin_ref, q_ref, k_ref, v_ref, row0, rows)
            moves += [(src.at[at], dst.at[at]) for src, dst in ((q_ref, q_hbm), (k_ref, k_hbm), (v_ref, v_hbm))]
        for n, (src, dst) in enumerate(moves):
            outs.append(pltpu.make_async_copy(src, dst, osem.at[g, n]))
            outs[-1].start()
    for copy in outs:
        copy.wait()


def block_call(layer, last, x, att, mlp_gain, w_o, w_gate, w_up, w_down, extra):
    rows, width = x.shape
    half = width // 2
    most = max(n for _, n in GROUPS)
    count = len(GROUPS)
    vmem = pl.BlockSpec(memory_space=pltpu.VMEM)
    hbm = pl.BlockSpec(memory_space=pl.ANY)
    out_shape = [jax.ShapeDtypeStruct((rows, width), BF16)]
    in_specs = [hbm, hbm, vmem, hbm, hbm, hbm, hbm]
    out_specs = [hbm]
    tables = []
    weights = [w_o, w_gate, w_up, w_down]
    if not last:
        in_specs += [vmem, hbm, hbm, hbm, hbm, hbm]
        weights += list(extra[3:])
        out_shape += [jax.ShapeDtypeStruct((rows, w.shape[2]), BF16) for w in extra[3:]]
        out_specs += [hbm] * 3
        tables = [pltpu.VMEM(extra[1].shape, F32)] * 2 + [pltpu.VMEM((rows, w.shape[2]), BF16) for w in extra[3:]]
    return pl.pallas_call(
        functools.partial(block_kernel, layer, last, GROUPS),
        name=f'block_{layer}',
        out_shape=out_shape,
        in_specs=in_specs,
        out_specs=out_specs,
        scratch_shapes=[
            pltpu.VMEM((rows, half), BF16),
            pltpu.VMEM(att.shape, BF16),
            pltpu.VMEM((2, rows, half), BF16),
            pltpu.VMEM((2, rows, half), BF16),
            pltpu.VMEM((rows, half), BF16),
            pltpu.VMEM((rows, half), BF16),
            pltpu.VMEM((2, rows, half), BF16),
            pltpu.VMEM((most, width), BF16),
            pltpu.VMEM((most, w_down.shape[1]), BF16),
        ] + [pltpu.VMEM(w.shape[1:], BF16) for w in weights] + tables + [
            pltpu.SemaphoreType.DMA((11,)),
            pltpu.SemaphoreType.DMA((count, 5)),
            pltpu.SemaphoreType.DMA((2, 2, count)),
            pltpu.SemaphoreType.DMA((2, 2, count)),
            pltpu.SemaphoreType.DMA((2, 2, count)),
        ],
        compiler_params=pltpu.CompilerParams(collective_id=layer, has_side_effects=True, vmem_limit_bytes=VMEM_LIMIT),
    )(x, att, mlp_gain, w_o, w_gate, w_up, w_down, *extra)


def solution(mesh):
    col_spec = P(None, None, 'tp')
    row_spec = P(None, 'tp', None)
    cache_spec = P(None, 'dp', 'tp', None, None)
    in_specs = (P('dp', None), P('dp'), P(), col_spec, col_spec, col_spec, row_spec, P(), col_spec, col_spec, row_spec, cache_spec, cache_spec)

    def body(x, lengths, attn_gain, w_q, w_k, w_v, w_o, mlp_gain, w_gate, w_up, w_down, k_cache, v_cache):
        layers = w_q.shape[0]
        order = length_order(lengths)
        q, k, v, cos, sin = qkv_call(lengths, x, attn_gain, w_q, w_k, w_v, k_cache.shape[-1])
        for layer in range(layers):
            last = layer == layers - 1
            att = attention_call(layer, lengths, order, q, k, v, k_cache, v_cache)
            extra = () if last else (attn_gain, cos, sin, w_q, w_k, w_v)
            x, *rest = block_call(layer, last, x, att, mlp_gain, w_o, w_gate, w_up, w_down, extra)
            if not last:
                q, k, v = rest
        return x

    return jax.shard_map(body, mesh=mesh, in_specs=in_specs, out_specs=P('dp', None), check_vma=False)
```

profile of v0, /device:TPU:0, one launch (start us, length us, event | category | flops | bytes accessed | tf_op | source)
XLA Modules:
  0.0 187.4 jit_solution(25404477592960351)
XLA Ops:
  0.0 0.7 compare_select_fusion
  0.7 0.2 convert_reduce_fusion
  0.8 0.7 select_reduce_fusion.order_ref
  1.5 9.6 %qkv_first.1 = (bf16[320,768]{1,0:T(8,128)(2,1)}, bf16[320,256]{1,0:T(8,128)(2,1)}, bf16[320,256]{1,0:T(8,128)(2,1)}, f32[320,128]{1,0:T(8,128)}, f32[320,128]{1,0:T(8,128)}) custom-call(s32[65]{0:T(128)} %len_ref.5, bf16[320,3072]{1,0:T(8,128)(2,1)} %refs_0_.1, bf16[2,3072]{1,0:T(2,128)(2,1)} %refs_7_.1, bf16[2,3072,768]{2,1,0:T(8,128)(2,1)} %refs_10_.1, ...), custom_call_target="tpu_custom_call" | custom-call | tf_op jit(solution)/shard_map/qkv_first/pallas_call | solution.py:114
  11.1 26.6 %attention_0.1.refs_1_ = bf16[320,768]{1,0:T(8,128)(2,1)} custom-call(s32[65]{0:T(128)} %len_ref.5, s32[65]{0:T(128)} %select_reduce_fusion.order_ref, bf16[320,768]{1,0:T(8,128)(2,1)} %get-tuple-element.14.q_hbm, bf16[320,256]{1,0:T(8,128)(2,1)} %get-tuple-element.15.k_hbm, bf16[320,256]{1,0:T(8,128)(2,1)} %get-tuple-element.16.v_hbm, ...), custom_call_target="tpu_custom_call" | custom-call | tf_op jit(solution)/shard_map/attention_0/pallas_call | solution.py:279
  37.7 63.3 %block_0.1 = (bf16[320,3072]{1,0:T(8,128)(2,1)}, bf16[320,768]{1,0:T(8,128)(2,1)}, bf16[320,256]{1,0:T(8,128)(2,1)}, bf16[320,256]{1,0:T(8,128)(2,1)}) custom-call(bf16[320,3072]{1,0:T(8,128)(2,1)} %refs_0_.1, bf16[320,768]{1,0:T(8,128)(2,1)} %attention_0.1.refs_1_, bf16[2,3072]{1,0:T(2,128)(2,1)} %refs_2_.3, bf16[2,768,3072]{2,1,0:T(8,128)(2,1)} %refs_3_.3, ...), custom_call_target="tpu_custom_call" | custom-call | tf_op jit(solution)/shard_map/block_0/pallas_call | solution.py:468
  101.1 26.0 %attention_1.1.refs_1_ = bf16[320,768]{1,0:T(8,128)(2,1)} custom-call(s32[65]{0:T(128)} %len_ref.5, s32[65]{0:T(128)} %select_reduce_fusion.order_ref, bf16[320,768]{1,0:T(8,128)(2,1)} %get-tuple-element.20.q_hbm, bf16[320,256]{1,0:T(8,128)(2,1)} %get-tuple-element.21.k_hbm, bf16[320,256]{1,0:T(8,128)(2,1)} %get-tuple-element.22.v_hbm, ...), custom_call_target="tpu_custom_call" | custom-call | tf_op jit(solution)/shard_map/attention_1/pallas_call | solution.py:279
  127.0 57.5 %block_1.1 = bf16[320,3072]{1,0:T(8,128)(2,1)} custom-call(bf16[320,3072]{1,0:T(8,128)(2,1)} %get-tuple-element.19.refs_0_, bf16[320,768]{1,0:T(8,128)(2,1)} %attention_1.1.refs_1_, bf16[2,3072]{1,0:T(2,128)(2,1)} %refs_2_.3, bf16[2,768,3072]{2,1,0:T(8,128)(2,1)} %refs_3_.3, bf16[2,3072,2048]{2,1,0:T(8,128)(2,1)} %refs_4_.3, bf16[2,3072,2048]{2,1,0:T(8,128)(2,1)} %refs_5_.3, ...), custom_call_target="tpu_custom_call" | custom-call | tf_op jit(solution)/shard_map/block_1/pallas_call | solution.py:468
  184.5 2.9 %copy.15 = bf16[320,3072]{1,0:T(8,128)(2,1)} copy(bf16[320,3072]{1,0:T(8,128)(2,1)} %block_1.1) | data formatting | bytes 3932160
where the time goes:
time: 186 us; the launch traced here: 187 us
  Pallas kernels  183 us (98%)
  local copies, waits for them, and re-layouts  2.94 us (2%)
    pallas_call x2, Pallas kernels, block_call(): pl.pallas_call(functools.partial(block_kernel, layer, last, GROUPS), name...  121 us
    pallas_call x2, Pallas kernels, attention_call(): pl.pallas_call(functools.partial(attention_kernel, layer), name=f'attenti...  52.5 us
    pallas_call x1, Pallas kernels, qkv_call(): pl.pallas_call(qkv_kernel, name='qkv_first', out_shape=[jax.ShapeDtypeStr...  9.64 us

commit v1 on v0

--- a/solution.py
+++ b/solution.py
@@ -23,7 +23,7 @@
 def rope_tables(len_ref, cos_ref, sin_ref):
     rows, head = cos_ref.shape
     dec_rows = len_ref.shape[0] - 1
-    block = 8
+    block = 32
     lane = lax.broadcasted_iota(jnp.int32, (block, head), 1)
     sub = lax.broadcasted_iota(jnp.int32, (block, head), 0)
     freq = jnp.exp(lax.rem(lane, head // 2).astype(F32) * (-2.0 / head * math.log(ROPE_BASE)))
@@ -179,12 +179,10 @@
     prefill = [pltpu.make_async_copy(src.at[layer, rows], dst, psems.at[n]) for n, (src, dst) in enumerate(((kc_hbm, kp), (vc_hbm, vp)))]
     for copy in prefill:
         copy.start()
-    for step in range(SLOTS - 1):
-        fetch(step, step)
-
     qs[...] = jnp.zeros_like(qs)
     for copy in fresh:
         copy.wait()
+    fetch(0, 0)
     for h in range(heads):
         qs[h // rep, pl.ds(h, rows, stride=8), :] = q_ref[0:rows, h * head:(h + 1) * head].astype(F32)
     kf[...] = k_ref[0:rows, :].astype(F32)
@@ -192,6 +190,8 @@
 
     for copy in prefill:
         copy.wait()
+    for step in range(1, SLOTS - 1):
+        fetch(step, step)
     limit = len_ref[rows]
 
     def prefill_head(h, _, keys):
@@ -320,8 +320,7 @@
     if not last:
         loads += [(wq_hbm.at[layer + 1], wq), (wk_hbm.at[layer + 1], wk), (wv_hbm.at[layer + 1], wv), (cos_hbm, cos_ref), (sin_hbm, sin_ref)]
     loads = [pltpu.make_async_copy(src, dst, lsem.at[n]) for n, (src, dst) in enumerate(loads)]
-    order = [1, 2, 0] + list(range(3, len(loads)))
-    for n in order:
+    for n in (1, 2, 0):
         loads[n].start()
 
     barrier = pltpu.get_barrier_semaphore()
@@ -393,6 +392,8 @@
 
     loads[1].wait()
     loads[2].wait()
+    for n in (3, 4, 5):
+        loads[n].start()
     for g in range(count):
         project(att, pl.ds(*groups[g]), wo, g)
         to_mate(0, g).start()
@@ -420,6 +421,8 @@
         lax.fori_loop(0, wg.shape[1] // TILE, up_tile, 0, unroll=2)
         if g == 0:
             loads[5].wait()
+            for copy in loads[6:]:
+                copy.start()
         project(act, pl.ds(0, rows), wd, g)
         to_mate(1, g).start()
         if g + 1 < count:

time: 186 us -> 174 us (0.935); the launches traced: 187 us -> 171 us
  Pallas kernels: 183 us -> 167 us
    pallas_call x2, Pallas kernels: 52.5 us -> 36.7 us  [attention_call(): pl.pallas_call(functools.partial(attention_kernel, layer), name=f'attenti...]
where the time goes in v1:
time: 174 us; the launch traced here: 171 us
  Pallas kernels  167 us (96%)
  local copies, waits for them, and re-layouts  2.94 us (2%)
    pallas_call x2, Pallas kernels, block_call(): pl.pallas_call(functools.partial(block_kernel, layer, last, GROUPS), name...  121 us
    pallas_call x2, Pallas kernels, attention_call(): pl.pallas_call(functools.partial(attention_kernel, layer), name=f'attenti...  36.7 us
    pallas_call x1, Pallas kernels, qkv_call(): pl.pallas_call(qkv_kernel, name='qkv_first', out_shape=[jax.ShapeDtypeStr...  9.13 us

profile of v1, /device:TPU:0, one launch (start us, length us, event | category | flops | bytes accessed | tf_op | source)
XLA Modules:
  0.0 171.1 jit_solution(18113019130389480350)
XLA Ops:
  0.0 0.7 compare_select_fusion
  0.7 0.2 convert_reduce_fusion
  0.8 0.7 select_reduce_fusion.order_ref
  1.5 9.1 %qkv_first.1 = (bf16[320,768]{1,0:T(8,128)(2,1)}, bf16[320,256]{1,0:T(8,128)(2,1)}, bf16[320,256]{1,0:T(8,128)(2,1)}, f32[320,128]{1,0:T(8,128)}, f32[320,128]{1,0:T(8,128)}) custom-call(s32[65]{0:T(128)} %len_ref.5, bf16[320,3072]{1,0:T(8,128)(2,1)} %refs_0_.1, bf16[2,3072]{1,0:T(2,128)(2,1)} %refs_7_.1, bf16[2,3072,768]{2,1,0:T(8,128)(2,1)} %refs_10_.1, ...), custom_call_target="tpu_custom_call" | custom-call | tf_op jit(solution)/shard_map/qkv_first/pallas_call | solution.py:114
  10.6 18.6 %attention_0.1.refs_1_ = bf16[320,768]{1,0:T(8,128)(2,1)} custom-call(s32[65]{0:T(128)} %len_ref.5, s32[65]{0:T(128)} %select_reduce_fusion.order_ref, bf16[320,768]{1,0:T(8,128)(2,1)} %get-tuple-element.14.q_hbm, bf16[320,256]{1,0:T(8,128)(2,1)} %get-tuple-element.15.k_hbm, bf16[320,256]{1,0:T(8,128)(2,1)} %get-tuple-element.16.v_hbm, ...), custom_call_target="tpu_custom_call" | custom-call | tf_op jit(solution)/shard_map/attention_0/pallas_call | solution.py:279
  29.2 63.3 %block_0.1 = (bf16[320,3072]{1,0:T(8,128)(2,1)}, bf16[320,768]{1,0:T(8,128)(2,1)}, bf16[320,256]{1,0:T(8,128)(2,1)}, bf16[320,256]{1,0:T(8,128)(2,1)}) custom-call(bf16[320,3072]{1,0:T(8,128)(2,1)} %refs_0_.1, bf16[320,768]{1,0:T(8,128)(2,1)} %attention_0.1.refs_1_, bf16[2,3072]{1,0:T(2,128)(2,1)} %refs_2_.3, bf16[2,768,3072]{2,1,0:T(8,128)(2,1)} %refs_3_.3, ...), custom_call_target="tpu_custom_call" | custom-call | tf_op jit(solution)/shard_map/block_0/pallas_call | solution.py:471
  92.6 18.1 %attention_1.1.refs_1_ = bf16[320,768]{1,0:T(8,128)(2,1)} custom-call(s32[65]{0:T(128)} %len_ref.5, s32[65]{0:T(128)} %select_reduce_fusion.order_ref, bf16[320,768]{1,0:T(8,128)(2,1)} %get-tuple-element.20.q_hbm, bf16[320,256]{1,0:T(8,128)(2,1)} %get-tuple-element.21.k_hbm, bf16[320,256]{1,0:T(8,128)(2,1)} %get-tuple-element.22.v_hbm, ...), custom_call_target="tpu_custom_call" | custom-call | tf_op jit(solution)/shard_map/attention_1/pallas_call | solution.py:279
  110.7 57.5 %block_1.1 = bf16[320,3072]{1,0:T(8,128)(2,1)} custom-call(bf16[320,3072]{1,0:T(8,128)(2,1)} %get-tuple-element.19.refs_0_, bf16[320,768]{1,0:T(8,128)(2,1)} %attention_1.1.refs_1_, bf16[2,3072]{1,0:T(2,128)(2,1)} %refs_2_.3, bf16[2,768,3072]{2,1,0:T(8,128)(2,1)} %refs_3_.3, bf16[2,3072,2048]{2,1,0:T(8,128)(2,1)} %refs_4_.3, bf16[2,3072,2048]{2,1,0:T(8,128)(2,1)} %refs_5_.3, ...), custom_call_target="tpu_custom_call" | custom-call | tf_op jit(solution)/shard_map/block_1/pallas_call | solution.py:471
  168.2 2.9 %copy.15 = bf16[320,3072]{1,0:T(8,128)(2,1)} copy(bf16[320,3072]{1,0:T(8,128)(2,1)} %block_1.1) | data formatting | bytes 3932160

commit v2 on v1

--- a/solution.py
+++ b/solution.py
@@ -17,7 +17,7 @@
 TILE = 256
 DOWN_TILE = 512
 SLOTS = 3
-GROUPS = ((0, 112), (112, 112), (224, 96))
+GROUPS = ((0, 128), (128, 96), (224, 96))
 
 
 def rope_tables(len_ref, cos_ref, sin_ref):
@@ -48,6 +48,26 @@
 
     lax.fori_loop(0, dec_rows // block, decode, 0)
     lax.fori_loop(dec_rows // block, rows // block, prefill, 0)
+
+
+def length_order(len_ref, order_ref):
+    rows = len_ref.shape[0] - 1
+    size = order_ref.shape[1]
+    sub8 = lax.broadcasted_iota(jnp.int32, (8, size), 0)
+    blocks = []
+    for i in range(size // 8):
+        block = jnp.full((8, size), -1, jnp.int32)
+        for r in range(i * 8, min(i * 8 + 8, rows)):
+            block = jnp.where(sub8 == r - i * 8, len_ref[r], block)
+        blocks.append(block.astype(F32))
+    mine = jnp.concatenate(blocks, axis=0)
+    other = mine.T
+    sub = lax.broadcasted_iota(jnp.int32, (size, size), 0)
+    lane = lax.broadcasted_iota(jnp.int32, (size, size), 1)
+    ahead = (other > mine) | ((other == mine) & (lane < sub))
+    rank = jnp.sum(jnp.where(ahead, 1.0, 0.0), axis=1, keepdims=True)
+    order = jnp.sum(jnp.where(rank == lane.astype(F32), sub.astype(F32), 0.0), axis=0, keepdims=True)
+    order_ref[...] = order.astype(jnp.int32)
 
 
 def norm_rows(h_ref, gain, b_ref, row0, rows, block=16):
@@ -64,7 +84,7 @@
         b_ref[dst, half:] = (hi * inv * gain_hi).astype(BF16)
         return 0
 
-    lax.fori_loop(0, rows // block, step, 0)
+    lax.fori_loop(0, rows // block, step, 0, unroll=2)
 
 
 def rope_store(prod, cos, sin, out_ref, rows, col):
@@ -86,18 +106,19 @@
         rope_store(prod, cos_ref[rows_at, :], sin_ref[rows_at, :], q_ref, rows_at, col)
         return 0
 
-    lax.fori_loop(0, wq_ref.shape[1] // TILE, q_tile, 0)
+    lax.fori_loop(0, wq_ref.shape[1] // TILE, q_tile, 0, unroll=True)
     rope_store(jnp.dot(lhs, wk_ref[...], preferred_element_type=F32), cos, sin, k_ref, rows_at, 0)
     v_ref[rows_at, :] = jnp.dot(lhs, wv_ref[...], preferred_element_type=F32).astype(BF16)
 
 
-def qkv_kernel(len_ref, x_hbm, gain_ref, wq_hbm, wk_hbm, wv_hbm, q_ref, k_ref, v_ref, cos_ref, sin_ref, h, b, wq, wk, wv, sems):
+def qkv_kernel(len_ref, x_hbm, gain_ref, wq_hbm, wk_hbm, wv_hbm, q_ref, k_ref, v_ref, cos_ref, sin_ref, order_ref, h, b, wq, wk, wv, sems):
     half = h.shape[2]
     copies = [pltpu.make_async_copy(x_hbm.at[:, pl.ds(s * half, half)], h.at[s], sems.at[s]) for s in range(2)]
     copies += [pltpu.make_async_copy(src.at[0], dst, sems.at[2 + n]) for n, (src, dst) in enumerate(((wq_hbm, wq), (wk_hbm, wk), (wv_hbm, wv)))]
     for copy in copies:
         copy.start()
     rope_tables(len_ref, cos_ref, sin_ref)
+    length_order(len_ref, order_ref)
     copies[0].wait()
     copies[1].wait()
     rows = h.shape[1]
@@ -114,9 +135,9 @@
     return pl.pallas_call(
         qkv_kernel,
         name='qkv_first',
-        out_shape=[jax.ShapeDtypeStruct((rows, w.shape[2]), BF16) for w in (w_q, w_k, w_v)] + [jax.ShapeDtypeStruct((rows, head), F32)] * 2,
+        out_shape=[jax.ShapeDtypeStruct((rows, w.shape[2]), BF16) for w in (w_q, w_k, w_v)] + [jax.ShapeDtypeStruct((rows, head), F32)] * 2 + [jax.ShapeDtypeStruct((1, 128), jnp.int32)],
         in_specs=[pl.BlockSpec(memory_space=pltpu.SMEM), hbm, vmem, hbm, hbm, hbm],
-        out_specs=[vmem] * 5,
+        out_specs=[vmem] * 6,
         scratch_shapes=[
             pltpu.VMEM((2, rows, width // 2), BF16),
             pltpu.VMEM((rows, width), BF16),
@@ -133,15 +154,6 @@
 SPAN = 256
 
 
-def length_order(lengths):
-    ids = jnp.arange(lengths.shape[0], dtype=jnp.int32)
-    lengths = jnp.where(ids == lengths.shape[0] - 1, 0, lengths)
-    mine, other = lengths[:, None], lengths[None, :]
-    ahead = (other > mine) | ((other == mine) & (ids[None, :] < ids[:, None]))
-    rank = jnp.sum(ahead.astype(jnp.int32), axis=1)
-    return jnp.sum(jnp.where(rank[None, :] == ids[:, None], ids[None, :], 0), axis=1)
-
-
 def attention_kernel(layer, len_ref, order_ref, q_hbm, k_hbm, v_hbm, kc_hbm, vc_hbm, o_ref, q_ref, k_ref, v_ref, kbuf, vbuf, qs, kf, vf, sc, od, kp, vp, sems, psems):
     rows = kc_hbm.shape[1] - 1
     seq, head = kc_hbm.shape[3], kc_hbm.shape[4]
@@ -154,12 +166,12 @@
     nt = (((1,), (1,)), ((), ()))
 
     def step_spans(step):
-        return len_ref[order_ref[step * BATCH]] // SPAN + 1
+        return len_ref[order_ref[0, step * BATCH]] // SPAN + 1
 
     def copies(step, slot, n, act):
         at = pl.ds(0, n * SPAN)
         for i in range(BATCH):
-            row = order_ref[step * BATCH + i]
+            row = order_ref[0, step * BATCH + i]
             for m, (src, dst) in enumerate(((kc_hbm, kbuf), (vc_hbm, vbuf))):
                 copy = pltpu.make_async_copy(src.at[layer, row, :, at, :], dst.at[slot, i, :, at, :], sems.at[slot, i, m])
                 if act == 'start':
@@ -221,7 +233,7 @@
         keys = n * SPAN
         copies(step, slot, n, 'wait')
         for i in range(BATCH):
-            row = order_ref[step * BATCH + i]
+            row = order_ref[0, step * BATCH + i]
             length = len_ref[row]
             base = pl.multiple_of((length // 16) * 16, 16)
             hit = lax.broadcasted_iota(jnp.int32, (16, head), 0) == length - base
@@ -233,7 +245,7 @@
                     mine = jnp.sum(jnp.where(pick, new[near, g * head:(g + 1) * head], 0.0), axis=0, keepdims=True)
                     buf[slot, i, g, pl.ds(base, 16), :] = jnp.where(hit, mine, old).astype(BF16)
         for i in range(BATCH):
-            row = order_ref[step * BATCH + i]
+            row = order_ref[0, step * BATCH + i]
             at = pl.ds(pl.multiple_of(row * 8, 8), 8)
             q = jnp.concatenate([qs[g, at, :] for g in range(kv)], axis=-1).astype(BF16)
             key = jnp.concatenate([kbuf[slot, i, g, 0:keys, :] for g in range(kv)], axis=-1)
@@ -250,7 +262,7 @@
             pick = o[:, 0:head]
             for g in range(1, kv):
                 pick = jnp.where(own == g, o[:, g * head:(g + 1) * head], pick)
-            row = order_ref[step * BATCH + i]
+            row = order_ref[0, step * BATCH + i]
             od[pl.ds(pl.multiple_of(row * 8, 8), 8), :] = pick
 
     def decode_step(step, _):
@@ -364,7 +376,7 @@
             send[at, :] = (part[core, at, :].astype(F32) + got[at, :].astype(F32)).astype(BF16)
             return 0
 
-        lax.fori_loop(0, rows // 16, step, 0)
+        lax.fori_loop(0, rows // 16, step, 0, unroll=2)
 
     def add_sum(phase, g):
         row0, rows = groups[g]
@@ -376,7 +388,7 @@
             h[core, at, :] = (base.astype(F32) + total).astype(BF16)
             return 0
 
-        lax.fori_loop(0, rows // 16, step, 0)
+        lax.fori_loop(0, rows // 16, step, 0, unroll=2)
 
     count = len(groups)
 
@@ -503,8 +515,7 @@
 
     def body(x, lengths, attn_gain, w_q, w_k, w_v, w_o, mlp_gain, w_gate, w_up, w_down, k_cache, v_cache):
         layers = w_q.shape[0]
-        order = length_order(lengths)
-        q, k, v, cos, sin = qkv_call(lengths, x, attn_gain, w_q, w_k, w_v, k_cache.shape[-1])
+        q, k, v, cos, sin, order = qkv_call(lengths, x, attn_gain, w_q, w_k, w_v, k_cache.shape[-1])
         for layer in range(layers):
             last = layer == layers - 1
             att = attention_call(layer, lengths, order, q, k, v, k_cache, v_cache)

time: 174 us -> 170 us (0.977); the launches traced: 171 us -> 170 us
    pallas_call x2, Pallas kernels: 36.7 us -> 41.2 us  [attention_call(): pl.pallas_call(functools.partial(attention_kernel, layer), name=f'attenti...]
    pallas_call x2, Pallas kernels: 121 us -> 118 us  [block_call(): pl.pallas_call(functools.partial(block_kernel, layer, last, GROUPS), name...]
where the time goes in v2:
time: 170 us
  Pallas kernels  167 us (98%)
  local copies, waits for them, and re-layouts  2.94 us (2%)
    pallas_call x2, Pallas kernels, block_call(): pl.pallas_call(functools.partial(block_kernel, layer, last, GROUPS), name...  118 us
    pallas_call x2, Pallas kernels, attention_call(): pl.pallas_call(functools.partial(attention_kernel, layer), name=f'attenti...  41.2 us
    pallas_call x1, Pallas kernels, qkv_call(): pl.pallas_call(qkv_kernel, name='qkv_first', out_shape=[jax.ShapeDtypeStr...  8.14 us

profile of v2, /device:TPU:0, one launch (start us, length us, event | category | flops | bytes accessed | tf_op | source)
XLA Modules:
  0.0 170.2 jit_solution(16393707517316630187)
XLA Ops:
  0.0 8.1 %qkv_first.1 = (bf16[320,768]{1,0:T(8,128)(2,1)}, bf16[320,256]{1,0:T(8,128)(2,1)}, bf16[320,256]{1,0:T(8,128)(2,1)}, f32[320,128]{1,0:T(8,128)}, f32[320,128]{1,0:T(8,128)}, /*index=5*/s32[1,128]{1,0:T(1,128)}) custom-call(s32[65]{0:T(128)} %len_ref.5, bf16[320,3072]{1,0:T(8,128)(2,1)} %refs_0_.1, bf16[2,3072]{1,0:T(2,128)(2,1)} %refs_7_.1, ...), custom_call_target="tpu_custom_call" | custom-call | tf_op jit(solution)/shard_map/qkv_first/pallas_call | solution.py:135
  8.2 20.9 %attention_0.1.refs_1_ = bf16[320,768]{1,0:T(8,128)(2,1)} custom-call(s32[65]{0:T(128)} %len_ref.5, s32[1,128]{1,0:T(1,128)} %get-tuple-element.15.order_ref, bf16[320,768]{1,0:T(8,128)(2,1)} %get-tuple-element.16.q_hbm, bf16[320,256]{1,0:T(8,128)(2,1)} %get-tuple-element.17.k_hbm, bf16[320,256]{1,0:T(8,128)(2,1)} %get-tuple-element.18.v_hbm, ...), custom_call_target="tpu_custom_call" | custom-call | tf_op jit(solution)/shard_map/attention_0/pallas_call | solution.py:291
  29.1 60.2 %block_0.1 = (bf16[320,3072]{1,0:T(8,128)(2,1)}, bf16[320,768]{1,0:T(8,128)(2,1)}, bf16[320,256]{1,0:T(8,128)(2,1)}, bf16[320,256]{1,0:T(8,128)(2,1)}) custom-call(bf16[320,3072]{1,0:T(8,128)(2,1)} %refs_0_.1, bf16[320,768]{1,0:T(8,128)(2,1)} %attention_0.1.refs_1_, bf16[2,3072]{1,0:T(2,128)(2,1)} %refs_2_.3, bf16[2,768,3072]{2,1,0:T(8,128)(2,1)} %refs_3_.3, ...), custom_call_target="tpu_custom_call" | custom-call | tf_op jit(solution)/shard_map/block_0/pallas_call | solution.py:483
  89.3 20.3 %attention_1.1.refs_1_ = bf16[320,768]{1,0:T(8,128)(2,1)} custom-call(s32[65]{0:T(128)} %len_ref.5, s32[1,128]{1,0:T(1,128)} %get-tuple-element.15.order_ref, bf16[320,768]{1,0:T(8,128)(2,1)} %get-tuple-element.22.q_hbm, bf16[320,256]{1,0:T(8,128)(2,1)} %get-tuple-element.23.k_hbm, bf16[320,256]{1,0:T(8,128)(2,1)} %get-tuple-element.24.v_hbm, ...), custom_call_target="tpu_custom_call" | custom-call | tf_op jit(solution)/shard_map/attention_1/pallas_call | solution.py:291
  109.6 57.6 %block_1.1 = bf16[320,3072]{1,0:T(8,128)(2,1)} custom-call(bf16[320,3072]{1,0:T(8,128)(2,1)} %get-tuple-element.21.refs_0_, bf16[320,768]{1,0:T(8,128)(2,1)} %attention_1.1.refs_1_, bf16[2,3072]{1,0:T(2,128)(2,1)} %refs_2_.3, bf16[2,768,3072]{2,1,0:T(8,128)(2,1)} %refs_3_.3, bf16[2,3072,2048]{2,1,0:T(8,128)(2,1)} %refs_4_.3, bf16[2,3072,2048]{2,1,0:T(8,128)(2,1)} %refs_5_.3, ...), custom_call_target="tpu_custom_call" | custom-call | tf_op jit(solution)/shard_map/block_1/pallas_call | solution.py:483
  167.2 2.9 %copy.15 = bf16[320,3072]{1,0:T(8,128)(2,1)} copy(bf16[320,3072]{1,0:T(8,128)(2,1)} %block_1.1) | data formatting | bytes 3932160
